TPU v7x, 32 devices: a whole 2x2x4 slice. The times are simulated.
32 devices in a mesh: member: 2 (over x), gx: 16 (over z, y, core).
Axes of the slice: x: 2, y: 2, z: 4, core: 2. Of those that a mesh axis runs over, the one named last changes fastest.
Arguments:
- spectrum: float32 [36, 32, 256, 128], P(None, None, ('member', 'gx')), parts along dimension 2, may hold values from 0 to 1
- wind: float32 [2, 256, 128], P(None, ('member', 'gx')), parts along dimension 1, may hold values from -32 to 32
- land_sea: int32 [128, 128], P('gx'), may hold values 0 or 1
- band_rows: int32 [128], replicated, may hold values from 0 to 127, each once
Outputs:
- spectrum_next: float32 [36, 32, 256, 128], P(None, None, ('member', 'gx')), parts along dimension 2
- ocean_fields: float32 [4, 128, 256], P(None, 'gx', 'member'), parts along dimension 2
There are 2 independent parts, one for each index of `member`. A program takes and returns all parts, laid end to end along the dimension named above; an argument that names none is the same for every part. Nothing has to cross between parts.
Inputs may be any that keep to these rules, and one draw needn't show every extreme that they name: band_rows names each of the 128 latitude rows exactly once.
All inputs are finite; a program needn't handle non-finite values. No bound on the sum of `land_sea` on one device may be relied on, other than what follows from the above.
Results may differ from a plain program's by a relative error of at most 0.00015.
Values sent between devices are 32-bit elements; how exact they have to be, the bound alone decides.
A program may use at most 128 MiB of HBM per device.

v0:
```python
import functools
import math

import jax
import jax.numpy as jnp
from jax import lax
from jax.experimental import pallas as pl
from jax.experimental.pallas import tpu as pltpu
from jax.sharding import PartitionSpec as P

STEPS = 3
SUB = 8
LEFT, RIGHT = 8, 10


def kernel(n, dirs, groups, spec, wind_in, land_in, bands_in, out, recv,
           trig, freq, wind, land, bands, x_ref, w_ref, g_ref, send_e, send_w, halo_l, halo_r, wind_h, land_h,
           wind_b, mask_b, r_ref, drift_ref, e_send, e_halo, rows, sends,
           in_sem, small_sem, col_sem, ssem, rsem, a_ssem, a_rsem):
    me = lax.axis_index("gx")
    right, left = lax.rem(me + 1, n), lax.rem(me + n - 1, n)
    quarter = dirs // 4
    qbins = quarter * groups * SUB
    cells = dirs * groups * SUB
    lane = lax.broadcasted_iota(jnp.int32, (SUB, 128), 1)
    x_rows = x_ref.reshape(cells * SUB, 128)

    def in_copy(q):
        part = pl.ds(q * qbins, qbins)
        return pltpu.make_async_copy(spec.at[part], x_ref.at[part], in_sem.at[q])

    def column_copies(k):
        copies = []
        for j, (first, bins, target, to, column) in enumerate([
                (0, qbins, send_e, 0, SUB - 1 - k), (3 * qbins, qbins, send_e, qbins, SUB - 1 - k),
                (qbins, 2 * qbins, send_w, 0, k)]):
            copies.append(pltpu.make_async_copy(
                spec.at[pl.ds(first, bins), column], target.at[k, pl.ds(to, bins)], col_sem.at[k, j]))
        return copies

    tables_in = [pltpu.make_async_copy(src, dst, small_sem.at[i]) for i, (src, dst) in enumerate(
        [(wind_in, wind), (land_in, land), (bands_in, bands)])]
    columns_in = [column_copies(k) for k in range(3)]
    for copy in columns_in[0] + tables_in:
        copy.start()
    for q in (0, 3, 1, 2):
        in_copy(q).start()
    for copy in columns_in[1] + columns_in[2]:
        copy.start()

    for d in range(dirs):
        angle = (d + 0.5) * (2.0 * math.pi / dirs)
        trig[0, d] = jnp.float32(math.cos(angle))
        trig[1, d] = jnp.float32(math.sin(angle))
    freqs = groups * SUB
    for f in range(groups):
        level = (lax.broadcasted_iota(jnp.int32, (SUB, 128), 0) + f * SUB).astype(jnp.float32)
        weight = (level + 1.0) * (1.0 / freqs)
        grown = jnp.exp(level * math.log(1.1))
        freq[0, f] = 0.45 / grown
        freq[1, f] = grown * (2.0 * math.pi * 0.0418 / 9.81)
        freq[2, f] = 0.3 * weight * weight
        freq[3, f] = weight * (3.0 / math.sqrt(dirs * freqs))

    barrier = pltpu.get_barrier_semaphore()

    def greet(i, _):
        pl.semaphore_signal(barrier, inc=1, device_id={"gx": lax.rem(me + i, n)},
                            device_id_type=pl.DeviceIdType.MESH)
        return 0

    lax.fori_loop(1, n, greet, 0)

    def remote(src, dst, slot, target):
        return pltpu.make_async_remote_copy(
            src_ref=src, dst_ref=dst, send_sem=ssem.at[slot], recv_sem=rsem.at[slot],
            device_id={"gx": target}, device_id_type=pl.DeviceIdType.MESH)

    bulk_e = [remote(send_e.at[k], halo_l.at[k], k, right) for k in range(3)]
    bulk_w = [remote(send_w.at[k], halo_r.at[k], 3 + k, left) for k in range(3)]
    small = [remote(wind, wind_h.at[0], 6, right), remote(wind, wind_h.at[1], 7, left),
             remote(land, land_h.at[0], 8, right), remote(land, land_h.at[1], 9, left)]
    energy_msg = [[remote(e_send.at[s], e_halo.at[s, 0], 10 + 2 * s, right),
                   remote(e_send.at[s], e_halo.at[s, 1], 11 + 2 * s, left)] for s in range(2)]

    for copy in columns_in[0]:
        copy.wait()
    pl.semaphore_wait(barrier, n - 1)
    for copy in [bulk_e[0], bulk_w[0]]:
        copy.start()
    for copy in tables_in:
        copy.wait()

    def spread(slot, wind_tile, land_tile, column):
        for c in range(2):
            wind_b[c, slot] = jnp.broadcast_to(wind_tile[c][column:column + 1], (SUB, 128))
        mask_b[slot] = jnp.broadcast_to(
            land_tile[column:column + 1].astype(jnp.float32), (SUB, 128))

    own_wind = [wind[0], wind[1]]
    own_land = land[...]
    for x in range(SUB):
        spread(x, own_wind, own_land, x)

    for copy in small:
        copy.start()
    for copy in columns_in[1] + columns_in[2]:
        copy.wait()
    for copy in [bulk_e[1], bulk_w[1]]:
        copy.start()
    for q in (0, 3, 1, 2):
        in_copy(q).wait()

    def scalars(d):
        return trig[0, d], trig[1, d]

    halves = [(0, 2 * quarter, True), (quarter, 0, False)]

    def coefficients(cosine, sine, f, east, turn):
        k = freq[0, f]
        along_x = k * (cosine if east else -cosine)
        along_y = k * jnp.abs(sine)
        centre = 1.0 - along_x - along_y
        return centre, along_x, jnp.where(lane == 127 * turn, 0.0, along_y)

    def shifted(value, turn):
        return pltpu.roll(value, 1 + 126 * turn, 1)

    def growth_of(cosine, sine, f, slot):
        ratio = (wind_b[0, slot] * cosine + wind_b[1, slot] * sine) * freq[1, f]
        return 0.05 * jnp.minimum(jnp.maximum(ratio - 1.0, 0.0), 4.0)

    zero = jnp.zeros((SUB, 128), jnp.float32)

    def main(step, sums):
        for d0, skip, east in halves:
            def body(i, sums, d0=d0, skip=skip, east=east):
                turn = i // quarter
                d = d0 + i + skip * turn
                cosine, sine = scalars(d)
                sums = list(sums)
                if step == 0:
                    speed = [wind_b[0, x] * cosine + wind_b[1, x] * sine for x in range(SUB)]
                for f in range(groups):
                    centre, along_x, along_y = coefficients(cosine, sine, f, east, turn)
                    before = None
                    for x in (range(SUB) if east else range(SUB - 1, -1, -1)):
                        at = (d * groups + f) * SUB + x
                        if step == 0:
                            value = x_rows[pl.ds((d * groups + f) * SUB * SUB + x, SUB, stride=SUB), :]
                            g_ref[at] = 0.05 * jnp.minimum(
                                jnp.maximum(speed[x] * freq[1, f] - 1.0, 0.0), 4.0)
                        else:
                            value = w_ref[at] * (1.0 + g_ref[at]) * r_ref[x, f]
                        new = centre * value + along_y * shifted(value, turn)
                        if before is not None:
                            new = new + along_x * before
                        before = value
                        w_ref[at] = new
                        sums[x] = sums[x] + new
                return tuple(sums)

            sums = lax.fori_loop(0, 2 * quarter, body, tuple(sums), unroll=2)
        return sums

    def fix(step, sums):
        first, last = sums[0], sums[SUB - 1]
        for d0, skip, east in halves:
            halo = halo_l if east else halo_r
            slot = LEFT if east else RIGHT
            edge = 0 if east else SUB - 1

            def body(i, total, d0=d0, skip=skip, east=east, halo=halo, slot=slot, edge=edge):
                turn = i // quarter
                d = d0 + i + skip * turn
                cosine, sine = scalars(d)
                for f in range(groups):
                    centre, along_x, along_y = coefficients(cosine, sine, f, east, turn)
                    at = i * groups + f

                    def advance(value, upwind, depth, s):
                        moved = centre * value + along_x * upwind + along_y * shifted(value, turn)
                        growth = growth_of(cosine, sine, f, slot + depth)
                        return moved * (1.0 + growth) * r_ref[slot + depth + 4 * (s if depth == 0 else 0), f]

                    if step == 0:
                        flow = halo[0, pl.ds(at * SUB, SUB), :]
                    elif step == 1:
                        flow = advance(halo[0, pl.ds(at * SUB, SUB), :], halo[1, pl.ds(at * SUB, SUB), :], 0, 0)
                        halo[0, pl.ds(at * SUB, SUB), :] = flow
                    else:
                        far = advance(halo[1, pl.ds(at * SUB, SUB), :], halo[2, pl.ds(at * SUB, SUB), :], 1, 0)
                        flow = advance(halo[0, pl.ds(at * SUB, SUB), :], far, 0, 1)
                    extra = along_x * flow
                    cell = (d * groups + f) * SUB + edge
                    w_ref[cell] = w_ref[cell] + extra
                    total = total + extra
                return total

            if east:
                first = lax.fori_loop(0, 2 * quarter, body, first, unroll=3)
            else:
                last = lax.fori_loop(0, 2 * quarter, body, last, unroll=3)
        return (first,) + tuple(sums[1:-1]) + (last,)

    def energy_tile(sums):
        return jnp.concatenate(
            [jnp.sum(s * mask_b[x], axis=0, keepdims=True) for x, s in enumerate(sums)],
            axis=0) * (1.0 / cells)

    def factor(tile, column, mask_slot, slot):
        ratio = jnp.broadcast_to(tile[column:column + 1], (SUB, 128))
        for f in range(groups):
            r_ref[slot, f] = mask_b[mask_slot] / (1.0 + freq[2, f] * ratio)

    def own_factors(tile):
        ratio = tile / (0.5 + tile)
        for x in range(SUB):
            factor(ratio, x, x, x)

    sums = main(0, (zero,) * SUB)
    for copy in small:
        copy.wait()
    for side in range(2):
        tiles = [wind_h[side, 0], wind_h[side, 1]]
        land_tile = land_h[side]
        for depth in range(2):
            spread((LEFT if side == 0 else RIGHT) + depth, tiles, land_tile,
                   SUB - 1 - depth if side == 0 else depth)
    bulk_e[0].wait()
    bulk_w[0].wait()
    sums = fix(0, sums)
    for step in (1, 2):
        tile = energy_tile(sums)
        e_send[step - 1] = tile
        own_factors(tile)
        for copy in energy_msg[step - 1]:
            copy.start()
        if step == 1:
            bulk_e[2].start()
            bulk_w[2].start()
        sums = main(step, (zero,) * SUB)
        bulk_e[step].wait()
        bulk_w[step].wait()
        for copy in energy_msg[step - 1]:
            copy.wait()
        for side in range(2):
            seen = e_halo[step - 1, side]
            ratio = seen / (0.5 + seen)
            base = LEFT if side == 0 else RIGHT
            for depth in range(3 - step):
                factor(ratio, SUB - 1 - depth if side == 0 else depth, base + depth,
                       base + depth + 4 * (step - 1))
        sums = fix(step, sums)

    own_factors(energy_tile(sums))

    def gather(d, carry):
        cosine, sine = scalars(d)
        carry = list(carry)
        for x in range(SUB):
            flux, drift = zero, zero
            for f in range(groups):
                at = (d * groups + f) * SUB + x
                moved = w_ref[at]
                flow = g_ref[at] * moved
                flux = flux + freq[3, f] * flow
                drift = drift + drift_ref[x, f] * (moved + flow)
            carry[x] = carry[x] + cosine * flux
            carry[SUB + x] = carry[SUB + x] + sine * flux
            carry[2 * SUB + x] = carry[2 * SUB + x] + cosine * drift
            carry[3 * SUB + x] = carry[3 * SUB + x] + sine * drift
        return tuple(carry)

    for x in range(SUB):
        for f in range(groups):
            drift_ref[x, f] = freq[3, f] * r_ref[x, f]
    carry = lax.fori_loop(0, dirs, gather, (zero,) * (4 * SUB), unroll=2)

    total = []
    for j, value in enumerate(carry):
        if j < 2 * SUB:
            value = value * mask_b[j % SUB]
        total.append(jnp.sum(value, axis=0, keepdims=True))
    total.append(jnp.zeros((128 - 4 * SUB, 128), jnp.float32))
    stacked = jnp.concatenate(total, axis=0)
    lat = lax.broadcasted_iota(jnp.int32, (128, 128), 0)
    pick = (lat == bands[...]).astype(jnp.float32)
    picked = jnp.dot(stacked, pick, precision=lax.Precision.HIGHEST,
                     preferred_element_type=jnp.float32)
    rows[...] = picked.T
    band = 128 // n
    for k in range(n):
        sends[k] = rows[pl.ds(k * band, band), :]

    def exchange(i):
        target = lax.rem(me + i, n)
        return pltpu.make_async_remote_copy(
            src_ref=sends.at[target], dst_ref=recv.at[me], send_sem=a_ssem.at[i],
            recv_sem=a_rsem.at[i], device_id={"gx": target},
            device_id_type=pl.DeviceIdType.MESH)

    def begin(i, _):
        exchange(i).start()
        return 0

    def finish(i, _):
        exchange(i).wait()
        return 0

    lax.fori_loop(1, n, begin, 0)
    recv[pl.ds(me, 1)] = sends[pl.ds(me, 1)]

    def write(d, _):
        for f in range(groups):
            for x in range(SUB):
                at = (d * groups + f) * SUB + x
                moved = w_ref[at]
                out[pl.ds((d * groups + f) * SUB * SUB + x, SUB, stride=SUB), :] = (
                    moved * (1.0 + g_ref[at]) * r_ref[x, f])
        return 0

    lax.fori_loop(0, dirs, write, 0, unroll=2)
    lax.fori_loop(1, n, finish, 0)


def finish_kernel(n, parts, out, recv, after, ocean_out, ocean, sem):
    rows = out.shape[0] // parts
    copies = []
    for q in range(parts):
        part = pl.ds(q * rows, rows)
        copies.append(pltpu.make_async_copy(out.at[part], after.at[part], sem.at[q]))
        copies[-1].start()
    band = 128 // n
    per_tile = 128 // SUB
    block = lax.broadcasted_iota(jnp.int32, (band, 128), 1) // SUB
    for tile in range(max(1, n // per_tile)):
        for c in range(4):
            built = jnp.zeros((band, 128), jnp.float32)
            for k in range(min(n, per_tile)):
                moved = pltpu.roll(recv[tile * per_tile + k], (SUB * (k - c)) % 128, 1)
                built = jnp.where(block == k, moved, built)
            ocean[c, :, tile * 128:(tile + 1) * 128] = built
    copies.append(pltpu.make_async_copy(ocean, ocean_out, sem.at[parts]))
    copies[-1].start()
    for copy in copies:
        copy.wait()


def per_device(n, spectrum, wind, land_sea, band_rows):
    dirs, freqs, columns, lats = spectrum.shape
    groups = freqs // SUB
    half = dirs // 2 * groups * SUB
    band = lats // n
    f32 = jnp.float32
    anywhere = pl.BlockSpec(memory_space=pltpu.HBM)
    vmem = pl.BlockSpec(memory_space=pltpu.VMEM)
    cells = dirs * groups * SUB
    after, recv = pl.pallas_call(
        functools.partial(kernel, n, dirs, groups),
        out_shape=(pltpu.VMEM((cells * SUB, lats), f32), pltpu.VMEM((n, band, 128), f32)),
        in_specs=[anywhere] * 4,
        out_specs=(vmem, vmem),
        scratch_shapes=[
            pltpu.SMEM((2, dirs), f32),
            pltpu.VMEM((4, groups, SUB, lats), f32),
            pltpu.VMEM((2, SUB, lats), f32),
            pltpu.VMEM((SUB, lats), jnp.int32),
            pltpu.VMEM((1, lats), jnp.int32),
            pltpu.VMEM((cells, SUB, lats), f32),
            pltpu.VMEM((cells, SUB, lats), f32),
            pltpu.VMEM((cells, SUB, lats), f32),
            pltpu.VMEM((3, half, lats), f32),
            pltpu.VMEM((3, half, lats), f32),
            pltpu.VMEM((3, half, lats), f32),
            pltpu.VMEM((3, half, lats), f32),
            pltpu.VMEM((2, 2, SUB, lats), f32),
            pltpu.VMEM((2, SUB, lats), jnp.int32),
            pltpu.VMEM((2, 12, SUB, lats), f32),
            pltpu.VMEM((12, SUB, lats), f32),
            pltpu.VMEM((16, groups, SUB, lats), f32),
            pltpu.VMEM((SUB, groups, SUB, lats), f32),
            pltpu.VMEM((2, SUB, lats), f32),
            pltpu.VMEM((2, 2, SUB, lats), f32),
            pltpu.VMEM((128, 128), f32),
            pltpu.VMEM((n, band, 128), f32),
            pltpu.SemaphoreType.DMA((4,)),
            pltpu.SemaphoreType.DMA((3,)),
            pltpu.SemaphoreType.DMA((3, 3)),
            pltpu.SemaphoreType.DMA((14,)),
            pltpu.SemaphoreType.DMA((14,)),
            pltpu.SemaphoreType.DMA((n,)),
            pltpu.SemaphoreType.DMA((n,)),
        ],
        compiler_params=pltpu.CompilerParams(
            collective_id=0, has_side_effects=True, vmem_limit_bytes=48 * 2**20),
        name="wave_window",
    )(*[pltpu.with_memory_space_constraint(a, pltpu.HBM) for a in (
        spectrum.reshape(cells, SUB, lats), wind, land_sea, band_rows.reshape(1, lats))])
    parts = 4
    after, ocean = pl.pallas_call(
        functools.partial(finish_kernel, n, parts),
        out_shape=(jax.ShapeDtypeStruct((cells * SUB, lats), f32),
                   jax.ShapeDtypeStruct((4, band, columns * n), f32)),
        in_specs=[vmem, vmem],
        out_specs=(anywhere, anywhere),
        scratch_shapes=[pltpu.VMEM((4, band, columns * n), f32), pltpu.SemaphoreType.DMA((parts + 1,))],
        compiler_params=pltpu.CompilerParams(vmem_limit_bytes=2**20),
        name="hand_over",
    )(after, recv)
    return after.reshape(spectrum.shape), ocean


def solution(mesh):
    placed = (
        P(None, None, ("member", "gx"), None),
        P(None, ("member", "gx"), None),
        P("gx", None),
        P(),
    )
    return jax.shard_map(
        functools.partial(per_device, mesh.shape["gx"]),
        mesh=mesh,
        in_specs=placed,
        out_specs=(P(None, None, ("member", "gx"), None), P(None, "gx", "member")),
        check_vma=False,
    )
```

profile of v0, /device:TPU:0, one launch (start us, length us, event | category | flops | bytes accessed | tf_op | source)
XLA Modules:
  0.0 39.6 jit_solution(17610640624613221146)
XLA Ops:
  0.6 36.7 %wave_window.1 = (f32[9216,128]{1,0:T(8,128)S(1)}, f32[16,8,128]{2,1,0:T(8,128)S(1)}) custom-call(f32[1152,8,128]{2,1,0:T(8,128)} %bitcast.3, f32[2,8,128]{2,1,0:T(8,128)} %wind_in.1, s32[8,128]{1,0:T(8,128)} %land_in.1, s32[1,128]{1,0:T(1,128)} %bitcast.4), custom_call_target="tpu_custom_call" | custom-call | tf_op jit(solution)/shard_map/wave_window/pallas_call | solution.py:359
  37.3 2.3 %hand_over.1 = (f32[9216,128]{1,0:T(8,128)}, f32[4,8,128]{2,1,0:T(8,128)}) custom-call(f32[9216,128]{1,0:T(8,128)S(1)} %get-tuple-element.6.out, f32[16,8,128]{2,1,0:T(8,128)S(1)} %get-tuple-element.7.recv), custom_call_target="tpu_custom_call" | custom-call | tf_op jit(solution)/shard_map/hand_over/pallas_call | solution.py:401
where the time goes:
time: 39.7 us; the launch traced here: 39.6 us
  Pallas kernels  38.9 us (98%)
  between operations  0.64 us (2%)
    pallas_call x1, Pallas kernels, per_device(): pl.pallas_call(functools.partial(kernel, n, dirs, groups), out_shape=(plt...  36.7 us
    pallas_call x1, Pallas kernels, per_device(): pl.pallas_call(functools.partial(finish_kernel, n, parts), out_shape=(jax...  2.25 us

commit v1 on v0

--- a/solution.py
+++ b/solution.py
@@ -14,37 +14,45 @@
 
 
 def kernel(n, dirs, groups, spec, wind_in, land_in, bands_in, out, recv,
-           trig, freq, wind, land, bands, x_ref, w_ref, g_ref, send_e, send_w, halo_l, halo_r, wind_h, land_h,
-           wind_b, mask_b, r_ref, drift_ref, e_send, e_halo, rows, sends,
-           in_sem, small_sem, col_sem, ssem, rsem, a_ssem, a_rsem):
+           trig, freq, wind, land, bands, x_ref, w_ref, g_ref, send, halo, wind_h, land_h,
+           wind_b, mask_b, r_ref, drift_ref, e_send, e_halo, rows, sends, coef,
+           in_sem, small_sem, col_sem, meet, bulk_s, bulk_r, small_s, small_r, e_s, e_r, a_s, a_r):
     me = lax.axis_index("gx")
     right, left = lax.rem(me + 1, n), lax.rem(me + n - 1, n)
+    late = lax.rem((me + 1) // 2, 2) == 0
+
+    def greet(semaphore, reach):
+        for peer in (lax.rem(me + reach, n), lax.rem(me + n - reach, n)):
+            pl.semaphore_signal(semaphore, inc=1, device_id={"gx": peer},
+                                device_id_type=pl.DeviceIdType.MESH)
+
+    barrier = pltpu.get_barrier_semaphore()
+    greet(barrier, 1)
+    reaches = [2 ** i for i in range((n // 2 - 1).bit_length())]
     quarter = dirs // 4
     qbins = quarter * groups * SUB
     cells = dirs * groups * SUB
     lane = lax.broadcasted_iota(jnp.int32, (SUB, 128), 1)
     x_rows = x_ref.reshape(cells * SUB, 128)
 
-    def in_copy(q):
-        part = pl.ds(q * qbins, qbins)
-        return pltpu.make_async_copy(spec.at[part], x_ref.at[part], in_sem.at[q])
+    in_copy = pltpu.make_async_copy(spec, x_ref, in_sem.at[0])
 
     def column_copies(k):
-        copies = []
-        for j, (first, bins, target, to, column) in enumerate([
-                (0, qbins, send_e, 0, SUB - 1 - k), (3 * qbins, qbins, send_e, qbins, SUB - 1 - k),
-                (qbins, 2 * qbins, send_w, 0, k)]):
-            copies.append(pltpu.make_async_copy(
-                spec.at[pl.ds(first, bins), column], target.at[k, pl.ds(to, bins)], col_sem.at[k, j]))
-        return copies
+        return [pltpu.make_async_copy(
+            spec.at[pl.ds(first, bins), column], send.at[k, side, pl.ds(to, bins)], col_sem.at[k])
+            for first, bins, side, to, column in [
+                (0, qbins, 0, 0, SUB - 1 - k), (3 * qbins, qbins, 0, qbins, SUB - 1 - k),
+                (qbins, 2 * qbins, 1, 0, k)]]
+
+    def columns_here(k):
+        pltpu.make_async_copy(send.at[k], halo.at[k], col_sem.at[k]).wait()
 
     tables_in = [pltpu.make_async_copy(src, dst, small_sem.at[i]) for i, (src, dst) in enumerate(
         [(wind_in, wind), (land_in, land), (bands_in, bands)])]
     columns_in = [column_copies(k) for k in range(3)]
     for copy in columns_in[0] + tables_in:
         copy.start()
-    for q in (0, 3, 1, 2):
-        in_copy(q).start()
+    in_copy.start()
     for copy in columns_in[1] + columns_in[2]:
         copy.start()
 
@@ -62,32 +70,27 @@
         freq[2, f] = 0.3 * weight * weight
         freq[3, f] = weight * (3.0 / math.sqrt(dirs * freqs))
 
-    barrier = pltpu.get_barrier_semaphore()
-
-    def greet(i, _):
-        pl.semaphore_signal(barrier, inc=1, device_id={"gx": lax.rem(me + i, n)},
-                            device_id_type=pl.DeviceIdType.MESH)
-        return 0
-
-    lax.fori_loop(1, n, greet, 0)
-
-    def remote(src, dst, slot, target):
+    def remote(src, dst, send_sem, recv_sem, target):
         return pltpu.make_async_remote_copy(
-            src_ref=src, dst_ref=dst, send_sem=ssem.at[slot], recv_sem=rsem.at[slot],
+            src_ref=src, dst_ref=dst, send_sem=send_sem, recv_sem=recv_sem,
             device_id={"gx": target}, device_id_type=pl.DeviceIdType.MESH)
 
-    bulk_e = [remote(send_e.at[k], halo_l.at[k], k, right) for k in range(3)]
-    bulk_w = [remote(send_w.at[k], halo_r.at[k], 3 + k, left) for k in range(3)]
-    small = [remote(wind, wind_h.at[0], 6, right), remote(wind, wind_h.at[1], 7, left),
-             remote(land, land_h.at[0], 8, right), remote(land, land_h.at[1], 9, left)]
-    energy_msg = [[remote(e_send.at[s], e_halo.at[s, 0], 10 + 2 * s, right),
-                   remote(e_send.at[s], e_halo.at[s, 1], 11 + 2 * s, left)] for s in range(2)]
-
-    for copy in columns_in[0]:
-        copy.wait()
-    pl.semaphore_wait(barrier, n - 1)
-    for copy in [bulk_e[0], bulk_w[0]]:
+    def arrived(ref, sem):
+        pltpu.make_async_copy(ref, ref, sem).wait()
+
+    bulk = [[remote(send.at[k, side], halo.at[k, side], bulk_s.at[0], bulk_r.at[k],
+                    (right, left)[side]) for side in range(2)] for k in range(3)]
+    small = [remote(src, dst.at[side], small_s.at[j], small_r.at[j], (right, left)[side])
+             for j, (src, dst) in enumerate([(wind, wind_h), (land, land_h)]) for side in range(2)]
+    energy_msg = [[remote(e_send.at[s], e_halo.at[s, side], e_s.at[s], e_r.at[s],
+                          (right, left)[side]) for side in range(2)] for s in range(2)]
+
+    columns_here(0)
+    pl.semaphore_wait(barrier, 2)
+    for copy in bulk[0]:
         copy.start()
+    if reaches:
+        greet(meet.at[0], reaches[0])
     for copy in tables_in:
         copy.wait()
 
@@ -104,12 +107,24 @@
 
     for copy in small:
         copy.start()
-    for copy in columns_in[1] + columns_in[2]:
-        copy.wait()
-    for copy in [bulk_e[1], bulk_w[1]]:
+    columns_here(1)
+    columns_here(2)
+
+    def launch(k, when):
+        @pl.when(when)
+        def _():
+            for copy in bulk[k]:
+                copy.start()
+
+    def spread_word(rounds):
+        for i in rounds:
+            pl.semaphore_wait(meet.at[i], 2)
+            if i + 1 < len(reaches):
+                greet(meet.at[i + 1], reaches[i + 1])
+
+    for copy in bulk[1]:
         copy.start()
-    for q in (0, 3, 1, 2):
-        in_copy(q).wait()
+    in_copy.wait()
 
     def scalars(d):
         return trig[0, d], trig[1, d]
@@ -163,50 +178,75 @@
             sums = lax.fori_loop(0, 2 * quarter, body, tuple(sums), unroll=2)
         return sums
 
-    def fix(step, sums):
-        first, last = sums[0], sums[SUB - 1]
-        for d0, skip, east in halves:
-            halo = halo_l if east else halo_r
-            slot = LEFT if east else RIGHT
-            edge = 0 if east else SUB - 1
-
-            def body(i, total, d0=d0, skip=skip, east=east, halo=halo, slot=slot, edge=edge):
+    def edges():
+        for side, (d0, skip, east) in enumerate(halves):
+            yield side, d0, skip, east, (LEFT if east else RIGHT), (0 if east else SUB - 1)
+
+    def over_tiles(body, carry, unroll=3):
+        return lax.fori_loop(0, 2 * quarter, body, carry, unroll=unroll)
+
+    def prepare(step):
+        for side, d0, skip, east, slot, edge in edges():
+            def body(i, carry, d0=d0, skip=skip, east=east, side=side, slot=slot):
                 turn = i // quarter
                 d = d0 + i + skip * turn
                 cosine, sine = scalars(d)
                 for f in range(groups):
                     centre, along_x, along_y = coefficients(cosine, sine, f, east, turn)
-                    at = i * groups + f
-
-                    def advance(value, upwind, depth, s):
-                        moved = centre * value + along_x * upwind + along_y * shifted(value, turn)
-                        growth = growth_of(cosine, sine, f, slot + depth)
-                        return moved * (1.0 + growth) * r_ref[slot + depth + 4 * (s if depth == 0 else 0), f]
-
+                    at = pl.ds((i * groups + f) * SUB, SUB)
+
+                    def local(k, depth):
+                        value = halo[k, side, at, :]
+                        grown = 1.0 + growth_of(cosine, sine, f, slot + depth)
+                        return (centre * value + along_y * shifted(value, turn)), grown
+
+                    near, grown = local(0, 0)
+                    if step == 1:
+                        halo[0, side, at, :] = near * grown
+                        coef[side, at, :] = along_x * grown
+                    else:
+                        far, grown_far = local(1, 1)
+                        grown = along_x * grown
+                        reach = along_x * grown_far * r_ref[slot + 1, f]
+                        halo[0, side, at, :] = grown * (near + reach * far)
+                        coef[side, at, :] = grown * reach * along_x
+                return carry
+
+            over_tiles(body, 0)
+
+    def fix(step, sums):
+        totals = {}
+        for side, d0, skip, east, slot, edge in edges():
+            def body(i, total, d0=d0, skip=skip, east=east, side=side, slot=slot, edge=edge):
+                turn = i // quarter
+                d = d0 + i + skip * turn
+                cosine, _ = scalars(d)
+                for f in range(groups):
+                    at = pl.ds((i * groups + f) * SUB, SUB)
+                    along_x = freq[0, f] * (cosine if east else -cosine)
                     if step == 0:
-                        flow = halo[0, pl.ds(at * SUB, SUB), :]
-                    elif step == 1:
-                        flow = advance(halo[0, pl.ds(at * SUB, SUB), :], halo[1, pl.ds(at * SUB, SUB), :], 0, 0)
-                        halo[0, pl.ds(at * SUB, SUB), :] = flow
+                        extra = along_x * halo[0, side, at, :]
                     else:
-                        far = advance(halo[1, pl.ds(at * SUB, SUB), :], halo[2, pl.ds(at * SUB, SUB), :], 1, 0)
-                        flow = advance(halo[0, pl.ds(at * SUB, SUB), :], far, 0, 1)
-                    extra = along_x * flow
+                        flow = r_ref[slot + 4 * (step - 1), f] * (
+                            halo[0, side, at, :] + coef[side, at, :] * halo[step, side, at, :])
+                        if step == 1:
+                            halo[0, side, at, :] = flow
+                            extra = along_x * flow
+                        else:
+                            extra = flow
                     cell = (d * groups + f) * SUB + edge
                     w_ref[cell] = w_ref[cell] + extra
                     total = total + extra
                 return total
 
-            if east:
-                first = lax.fori_loop(0, 2 * quarter, body, first, unroll=3)
-            else:
-                last = lax.fori_loop(0, 2 * quarter, body, last, unroll=3)
-        return (first,) + tuple(sums[1:-1]) + (last,)
+            totals[edge] = over_tiles(body, sums[edge])
+        return tuple(totals.get(x, sums[x]) for x in range(SUB))
+
+    def energy_rows(sums, which):
+        return [jnp.sum(sums[x] * mask_b[x], axis=0, keepdims=True) for x in which]
 
     def energy_tile(sums):
-        return jnp.concatenate(
-            [jnp.sum(s * mask_b[x], axis=0, keepdims=True) for x, s in enumerate(sums)],
-            axis=0) * (1.0 / cells)
+        return jnp.concatenate(energy_rows(sums, range(SUB)), axis=0) * (1.0 / cells)
 
     def factor(tile, column, mask_slot, slot):
         ratio = jnp.broadcast_to(tile[column:column + 1], (SUB, 128))
@@ -218,17 +258,40 @@
         for x in range(SUB):
             factor(ratio, x, x, x)
 
+    inner, outer = list(range(1, SUB - 1)), [0, SUB - 1]
+
+    def gathered(which, sums):
+        for x, row in zip(which, energy_rows(sums, which)):
+            tile = row * (1.0 / cells)
+            ratio = jnp.broadcast_to(tile / (0.5 + tile), (SUB, 128))
+            for f in range(groups):
+                value = mask_b[x] / (1.0 + freq[2, f] * ratio)
+                r_ref[x, f] = value
+                drift_ref[x, f] = freq[3, f] * value
+
+        def gather(d, carry):
+            cosine, sine = scalars(d)
+            carry = list(carry)
+            m = len(which)
+            for j, x in enumerate(which):
+                flux, drift = zero, zero
+                for f in range(groups):
+                    at = (d * groups + f) * SUB + x
+                    moved = w_ref[at]
+                    flow = g_ref[at] * moved
+                    flux = flux + freq[3, f] * flow
+                    drift = drift + drift_ref[x, f] * (moved + flow)
+                carry[j] = carry[j] + cosine * flux
+                carry[m + j] = carry[m + j] + sine * flux
+                carry[2 * m + j] = carry[2 * m + j] + cosine * drift
+                carry[3 * m + j] = carry[3 * m + j] + sine * drift
+            return tuple(carry)
+
+        return lax.fori_loop(0, dirs, gather, (zero,) * (4 * len(which)), unroll=2)
+
     sums = main(0, (zero,) * SUB)
-    for copy in small:
-        copy.wait()
-    for side in range(2):
-        tiles = [wind_h[side, 0], wind_h[side, 1]]
-        land_tile = land_h[side]
-        for depth in range(2):
-            spread((LEFT if side == 0 else RIGHT) + depth, tiles, land_tile,
-                   SUB - 1 - depth if side == 0 else depth)
-    bulk_e[0].wait()
-    bulk_w[0].wait()
+    spread_word(range(0, 1) if reaches else [])
+    arrived(halo.at[0], bulk_r.at[0])
     sums = fix(0, sums)
     for step in (1, 2):
         tile = energy_tile(sums)
@@ -236,14 +299,25 @@
         own_factors(tile)
         for copy in energy_msg[step - 1]:
             copy.start()
+        launch(2, late if step == 2 else jnp.logical_not(late))
+        sums = main(step, (zero,) * SUB)
         if step == 1:
-            bulk_e[2].start()
-            bulk_w[2].start()
-        sums = main(step, (zero,) * SUB)
-        bulk_e[step].wait()
-        bulk_w[step].wait()
-        for copy in energy_msg[step - 1]:
-            copy.wait()
+            spread_word(range(1, min(2, len(reaches))))
+            arrived(wind_h, small_r.at[0])
+            arrived(land_h, small_r.at[1])
+            for side in range(2):
+                tiles = [wind_h[side, 0], wind_h[side, 1]]
+                land_tile = land_h[side]
+                for depth in range(2):
+                    spread((LEFT if side == 0 else RIGHT) + depth, tiles, land_tile,
+                           SUB - 1 - depth if side == 0 else depth)
+        else:
+            spread_word(range(2, len(reaches)))
+        prepare(step)
+        if step == 2:
+            inner_sums = gathered(inner, sums)
+        arrived(halo.at[step], bulk_r.at[step])
+        arrived(e_halo.at[step - 1], e_r.at[step - 1])
         for side in range(2):
             seen = e_halo[step - 1, side]
             ratio = seen / (0.5 + seen)
@@ -253,29 +327,13 @@
                        base + depth + 4 * (step - 1))
         sums = fix(step, sums)
 
-    own_factors(energy_tile(sums))
-
-    def gather(d, carry):
-        cosine, sine = scalars(d)
-        carry = list(carry)
-        for x in range(SUB):
-            flux, drift = zero, zero
-            for f in range(groups):
-                at = (d * groups + f) * SUB + x
-                moved = w_ref[at]
-                flow = g_ref[at] * moved
-                flux = flux + freq[3, f] * flow
-                drift = drift + drift_ref[x, f] * (moved + flow)
-            carry[x] = carry[x] + cosine * flux
-            carry[SUB + x] = carry[SUB + x] + sine * flux
-            carry[2 * SUB + x] = carry[2 * SUB + x] + cosine * drift
-            carry[3 * SUB + x] = carry[3 * SUB + x] + sine * drift
-        return tuple(carry)
-
-    for x in range(SUB):
-        for f in range(groups):
-            drift_ref[x, f] = freq[3, f] * r_ref[x, f]
-    carry = lax.fori_loop(0, dirs, gather, (zero,) * (4 * SUB), unroll=2)
+    outer_sums = gathered(outer, sums)
+    both = {}
+    for which, parts in ((inner, inner_sums), (outer, outer_sums)):
+        for c in range(4):
+            for j, x in enumerate(which):
+                both[c * SUB + x] = parts[c * len(which) + j]
+    carry = [both[j] for j in range(4 * SUB)]
 
     total = []
     for j, value in enumerate(carry):
@@ -293,19 +351,9 @@
     for k in range(n):
         sends[k] = rows[pl.ds(k * band, band), :]
 
-    def exchange(i):
+    def begin(i, _):
         target = lax.rem(me + i, n)
-        return pltpu.make_async_remote_copy(
-            src_ref=sends.at[target], dst_ref=recv.at[me], send_sem=a_ssem.at[i],
-            recv_sem=a_rsem.at[i], device_id={"gx": target},
-            device_id_type=pl.DeviceIdType.MESH)
-
-    def begin(i, _):
-        exchange(i).start()
-        return 0
-
-    def finish(i, _):
-        exchange(i).wait()
+        remote(sends.at[target], recv.at[me], a_s.at[0], a_r.at[0], target).start()
         return 0
 
     lax.fori_loop(1, n, begin, 0)
@@ -321,7 +369,14 @@
         return 0
 
     lax.fori_loop(0, dirs, write, 0, unroll=2)
-    lax.fori_loop(1, n, finish, 0)
+    arrived(send, bulk_s.at[0])
+    arrived(wind_h, small_s.at[0])
+    arrived(land_h, small_s.at[1])
+    for s in range(2):
+        arrived(e_halo.at[s], e_s.at[s])
+    others = sends.at[pl.ds(0, n - 1)]
+    arrived(others, a_s.at[0])
+    arrived(others, a_r.at[0])
 
 
 def finish_kernel(n, parts, out, recv, after, ocean_out, ocean, sem):
@@ -370,10 +425,8 @@
             pltpu.VMEM((cells, SUB, lats), f32),
             pltpu.VMEM((cells, SUB, lats), f32),
             pltpu.VMEM((cells, SUB, lats), f32),
-            pltpu.VMEM((3, half, lats), f32),
-            pltpu.VMEM((3, half, lats), f32),
-            pltpu.VMEM((3, half, lats), f32),
-            pltpu.VMEM((3, half, lats), f32),
+            pltpu.VMEM((3, 2, half, lats), f32),
+            pltpu.VMEM((3, 2, half, lats), f32),
             pltpu.VMEM((2, 2, SUB, lats), f32),
             pltpu.VMEM((2, SUB, lats), jnp.int32),
             pltpu.VMEM((2, 12, SUB, lats), f32),
@@ -384,13 +437,19 @@
             pltpu.VMEM((2, 2, SUB, lats), f32),
             pltpu.VMEM((128, 128), f32),
             pltpu.VMEM((n, band, 128), f32),
-            pltpu.SemaphoreType.DMA((4,)),
+            pltpu.VMEM((2, half, lats), f32),
+            pltpu.SemaphoreType.DMA((1,)),
             pltpu.SemaphoreType.DMA((3,)),
-            pltpu.SemaphoreType.DMA((3, 3)),
-            pltpu.SemaphoreType.DMA((14,)),
-            pltpu.SemaphoreType.DMA((14,)),
-            pltpu.SemaphoreType.DMA((n,)),
-            pltpu.SemaphoreType.DMA((n,)),
+            pltpu.SemaphoreType.DMA((3,)),
+            pltpu.SemaphoreType.REGULAR((max(1, (n // 2 - 1).bit_length()),)),
+            pltpu.SemaphoreType.DMA((1,)),
+            pltpu.SemaphoreType.DMA((3,)),
+            pltpu.SemaphoreType.DMA((2,)),
+            pltpu.SemaphoreType.DMA((2,)),
+            pltpu.SemaphoreType.DMA((2,)),
+            pltpu.SemaphoreType.DMA((2,)),
+            pltpu.SemaphoreType.DMA((1,)),
+            pltpu.SemaphoreType.DMA((1,)),
         ],
         compiler_params=pltpu.CompilerParams(
             collective_id=0, has_side_effects=True, vmem_limit_bytes=48 * 2**20),

time: 39.7 us -> 36 us (0.907)
  Pallas kernels: 38.9 us -> 35.2 us
    pallas_call x1, Pallas kernels: 36.7 us -> 33 us  [per_device(): pl.pallas_call(functools.partial(kernel, n, dirs, groups), out_shape=(plt...]
where the time goes in v1:
time: 36 us; the launch traced here: 35.8 us
  Pallas kernels  35.2 us (98%)
  between operations  0.64 us (2%)
    pallas_call x1, Pallas kernels, per_device(): pl.pallas_call(functools.partial(kernel, n, dirs, groups), out_shape=(plt...  33 us
    pallas_call x1, Pallas kernels, per_device(): pl.pallas_call(functools.partial(finish_kernel, n, parts), out_shape=(jax...  2.25 us

profile of v1, /device:TPU:0, one launch (start us, length us, event | category | flops | bytes accessed | tf_op | source)
XLA Modules:
  0.0 35.8 jit_solution(4439550429146876305)
XLA Ops:
  0.6 33.0 %wave_window.1 = (f32[9216,128]{1,0:T(8,128)S(1)}, f32[16,8,128]{2,1,0:T(8,128)S(1)}) custom-call(f32[1152,8,128]{2,1,0:T(8,128)} %bitcast.3, f32[2,8,128]{2,1,0:T(8,128)} %wind_in.1, s32[8,128]{1,0:T(8,128)} %land_in.1, s32[1,128]{1,0:T(1,128)} %bitcast.4), custom_call_target="tpu_custom_call" | custom-call | tf_op jit(solution)/shard_map/wave_window/pallas_call | solution.py:414
  33.6 2.3 %hand_over.1 = (f32[9216,128]{1,0:T(8,128)}, f32[4,8,128]{2,1,0:T(8,128)}) custom-call(f32[9216,128]{1,0:T(8,128)S(1)} %get-tuple-element.6.out, f32[16,8,128]{2,1,0:T(8,128)S(1)} %get-tuple-element.7.recv), custom_call_target="tpu_custom_call" | custom-call | tf_op jit(solution)/shard_map/hand_over/pallas_call | solution.py:460

commit v2 on v1

--- a/solution.py
+++ b/solution.py
@@ -15,7 +15,7 @@
 
 def kernel(n, dirs, groups, spec, wind_in, land_in, bands_in, out, recv,
            trig, freq, wind, land, bands, x_ref, w_ref, g_ref, send, halo, wind_h, land_h,
-           wind_b, mask_b, r_ref, drift_ref, e_send, e_halo, rows, sends, coef,
+           wind_b, mask_b, r_ref, drift_ref, e_send, e_halo, rows, sends, coef, table, grow_h,
            in_sem, small_sem, col_sem, meet, bulk_s, bulk_r, small_s, small_r, e_s, e_r, a_s, a_r):
     me = lax.axis_index("gx")
     right, left = lax.rem(me + 1, n), lax.rem(me + n - 1, n)
@@ -87,12 +87,12 @@
 
     columns_here(0)
     pl.semaphore_wait(barrier, 2)
-    for copy in bulk[0]:
+    for copy in tables_in:
+        copy.wait()
+    for copy in small + bulk[0]:
         copy.start()
     if reaches:
         greet(meet.at[0], reaches[0])
-    for copy in tables_in:
-        copy.wait()
 
     def spread(slot, wind_tile, land_tile, column):
         for c in range(2):
@@ -105,8 +105,6 @@
     for x in range(SUB):
         spread(x, own_wind, own_land, x)
 
-    for copy in small:
-        copy.start()
     columns_here(1)
     columns_here(2)
 
@@ -138,6 +136,9 @@
         centre = 1.0 - along_x - along_y
         return centre, along_x, jnp.where(lane == 127 * turn, 0.0, along_y)
 
+    def stencil(bin_tile):
+        return table[0, bin_tile], table[1, bin_tile], table[2, bin_tile]
+
     def shifted(value, turn):
         return pltpu.roll(value, 1 + 126 * turn, 1)
 
@@ -152,21 +153,26 @@
             def body(i, sums, d0=d0, skip=skip, east=east):
                 turn = i // quarter
                 d = d0 + i + skip * turn
-                cosine, sine = scalars(d)
                 sums = list(sums)
                 if step == 0:
+                    cosine, sine = scalars(d)
                     speed = [wind_b[0, x] * cosine + wind_b[1, x] * sine for x in range(SUB)]
                 for f in range(groups):
-                    centre, along_x, along_y = coefficients(cosine, sine, f, east, turn)
+                    if step == 0:
+                        centre, along_x, along_y = coefficients(cosine, sine, f, east, turn)
+                        for c, value in enumerate((centre, along_x, along_y)):
+                            table[c, d * groups + f] = value
+                    else:
+                        centre, along_x, along_y = stencil(d * groups + f)
                     before = None
                     for x in (range(SUB) if east else range(SUB - 1, -1, -1)):
                         at = (d * groups + f) * SUB + x
                         if step == 0:
                             value = x_rows[pl.ds((d * groups + f) * SUB * SUB + x, SUB, stride=SUB), :]
-                            g_ref[at] = 0.05 * jnp.minimum(
+                            g_ref[at] = 1.0 + 0.05 * jnp.minimum(
                                 jnp.maximum(speed[x] * freq[1, f] - 1.0, 0.0), 4.0)
                         else:
-                            value = w_ref[at] * (1.0 + g_ref[at]) * r_ref[x, f]
+                            value = w_ref[at] * g_ref[at] * r_ref[x, f]
                         new = centre * value + along_y * shifted(value, turn)
                         if before is not None:
                             new = new + along_x * before
@@ -175,7 +181,7 @@
                         sums[x] = sums[x] + new
                 return tuple(sums)
 
-            sums = lax.fori_loop(0, 2 * quarter, body, tuple(sums), unroll=2)
+            sums = lax.fori_loop(0, 2 * quarter, body, tuple(sums), unroll=9)
         return sums
 
     def edges():
@@ -184,20 +190,32 @@
 
     def over_tiles(body, carry, unroll=3):
         return lax.fori_loop(0, 2 * quarter, body, carry, unroll=unroll)
+
+    def grow_halo():
+        for side, d0, skip, east, slot, edge in edges():
+            def body(i, carry, d0=d0, skip=skip, side=side, slot=slot):
+                d = d0 + i + skip * (i // quarter)
+                cosine, sine = scalars(d)
+                for f in range(groups):
+                    for depth in range(2):
+                        grow_h[side, depth, pl.ds((i * groups + f) * SUB, SUB), :] = (
+                            1.0 + growth_of(cosine, sine, f, slot + depth))
+                return carry
+
+            over_tiles(body, 0)
 
     def prepare(step):
         for side, d0, skip, east, slot, edge in edges():
             def body(i, carry, d0=d0, skip=skip, east=east, side=side, slot=slot):
                 turn = i // quarter
                 d = d0 + i + skip * turn
-                cosine, sine = scalars(d)
                 for f in range(groups):
-                    centre, along_x, along_y = coefficients(cosine, sine, f, east, turn)
+                    centre, along_x, along_y = stencil(d * groups + f)
                     at = pl.ds((i * groups + f) * SUB, SUB)
 
                     def local(k, depth):
                         value = halo[k, side, at, :]
-                        grown = 1.0 + growth_of(cosine, sine, f, slot + depth)
+                        grown = grow_h[side, depth, at, :]
                         return (centre * value + along_y * shifted(value, turn)), grown
 
                     near, grown = local(0, 0)
@@ -212,18 +230,16 @@
                         coef[side, at, :] = grown * reach * along_x
                 return carry
 
-            over_tiles(body, 0)
+            over_tiles(body, 0, 6)
 
     def fix(step, sums):
         totals = {}
         for side, d0, skip, east, slot, edge in edges():
             def body(i, total, d0=d0, skip=skip, east=east, side=side, slot=slot, edge=edge):
-                turn = i // quarter
-                d = d0 + i + skip * turn
-                cosine, _ = scalars(d)
+                d = d0 + i + skip * (i // quarter)
                 for f in range(groups):
                     at = pl.ds((i * groups + f) * SUB, SUB)
-                    along_x = freq[0, f] * (cosine if east else -cosine)
+                    along_x = table[1, d * groups + f]
                     if step == 0:
                         extra = along_x * halo[0, side, at, :]
                     else:
@@ -239,7 +255,7 @@
                     total = total + extra
                 return total
 
-            totals[edge] = over_tiles(body, sums[edge])
+            totals[edge] = over_tiles(body, sums[edge], 6)
         return tuple(totals.get(x, sums[x]) for x in range(SUB))
 
     def energy_rows(sums, which):
@@ -278,9 +294,9 @@
                 for f in range(groups):
                     at = (d * groups + f) * SUB + x
                     moved = w_ref[at]
-                    flow = g_ref[at] * moved
-                    flux = flux + freq[3, f] * flow
-                    drift = drift + drift_ref[x, f] * (moved + flow)
+                    grown = g_ref[at] * moved
+                    flux = flux + freq[3, f] * (grown - moved)
+                    drift = drift + drift_ref[x, f] * grown
                 carry[j] = carry[j] + cosine * flux
                 carry[m + j] = carry[m + j] + sine * flux
                 carry[2 * m + j] = carry[2 * m + j] + cosine * drift
@@ -291,6 +307,15 @@
 
     sums = main(0, (zero,) * SUB)
     spread_word(range(0, 1) if reaches else [])
+    arrived(wind_h, small_r.at[0])
+    arrived(land_h, small_r.at[1])
+    for side in range(2):
+        tiles = [wind_h[side, 0], wind_h[side, 1]]
+        land_tile = land_h[side]
+        for depth in range(2):
+            spread((LEFT if side == 0 else RIGHT) + depth, tiles, land_tile,
+                   SUB - 1 - depth if side == 0 else depth)
+    grow_halo()
     arrived(halo.at[0], bulk_r.at[0])
     sums = fix(0, sums)
     for step in (1, 2):
@@ -303,14 +328,6 @@
         sums = main(step, (zero,) * SUB)
         if step == 1:
             spread_word(range(1, min(2, len(reaches))))
-            arrived(wind_h, small_r.at[0])
-            arrived(land_h, small_r.at[1])
-            for side in range(2):
-                tiles = [wind_h[side, 0], wind_h[side, 1]]
-                land_tile = land_h[side]
-                for depth in range(2):
-                    spread((LEFT if side == 0 else RIGHT) + depth, tiles, land_tile,
-                           SUB - 1 - depth if side == 0 else depth)
         else:
             spread_word(range(2, len(reaches)))
         prepare(step)
@@ -365,7 +382,7 @@
                 at = (d * groups + f) * SUB + x
                 moved = w_ref[at]
                 out[pl.ds((d * groups + f) * SUB * SUB + x, SUB, stride=SUB), :] = (
-                    moved * (1.0 + g_ref[at]) * r_ref[x, f])
+                    moved * g_ref[at] * r_ref[x, f])
         return 0
 
     lax.fori_loop(0, dirs, write, 0, unroll=2)
@@ -438,6 +455,8 @@
             pltpu.VMEM((128, 128), f32),
             pltpu.VMEM((n, band, 128), f32),
             pltpu.VMEM((2, half, lats), f32),
+            pltpu.VMEM((3, dirs * groups, SUB, lats), f32),
+            pltpu.VMEM((2, 2, half, lats), f32),
             pltpu.SemaphoreType.DMA((1,)),
             pltpu.SemaphoreType.DMA((3,)),
             pltpu.SemaphoreType.DMA((3,)),

time: 36 us -> 34.4 us (0.956)
  Pallas kernels: 35.2 us -> 33.6 us
    pallas_call x1, Pallas kernels: 33 us -> 31.4 us  [per_device(): pl.pallas_call(functools.partial(kernel, n, dirs, groups), out_shape=(plt...]
where the time goes in v2:
time: 34.4 us; the launch traced here: 34.3 us
  Pallas kernels  33.6 us (98%)
  between operations  0.64 us (2%)
    pallas_call x1, Pallas kernels, per_device(): pl.pallas_call(functools.partial(kernel, n, dirs, groups), out_shape=(plt...  31.4 us
    pallas_call x1, Pallas kernels, per_device(): pl.pallas_call(functools.partial(finish_kernel, n, parts), out_shape=(jax...  2.25 us

profile of v2, /device:TPU:0, one launch (start us, length us, event | category | flops | bytes accessed | tf_op | source)
XLA Modules:
  0.0 34.3 jit_solution(17999512839685588550)
XLA Ops:
  0.6 31.4 %wave_window.1 = (f32[9216,128]{1,0:T(8,128)S(1)}, f32[16,8,128]{2,1,0:T(8,128)S(1)}) custom-call(f32[1152,8,128]{2,1,0:T(8,128)} %bitcast.3, f32[2,8,128]{2,1,0:T(8,128)} %wind_in.1, s32[8,128]{1,0:T(8,128)} %land_in.1, s32[1,128]{1,0:T(1,128)} %bitcast.4), custom_call_target="tpu_custom_call" | custom-call | tf_op jit(solution)/shard_map/wave_window/pallas_call | solution.py:431
  32.0 2.3 %hand_over.1 = (f32[9216,128]{1,0:T(8,128)}, f32[4,8,128]{2,1,0:T(8,128)}) custom-call(f32[9216,128]{1,0:T(8,128)S(1)} %get-tuple-element.6.out, f32[16,8,128]{2,1,0:T(8,128)S(1)} %get-tuple-element.7.recv), custom_call_target="tpu_custom_call" | custom-call | tf_op jit(solution)/shard_map/hand_over/pallas_call | solution.py:479

commit v3 on v2

--- a/solution.py
+++ b/solution.py
@@ -80,10 +80,14 @@
 
     bulk = [[remote(send.at[k, side], halo.at[k, side], bulk_s.at[0], bulk_r.at[k],
                     (right, left)[side]) for side in range(2)] for k in range(3)]
-    small = [remote(src, dst.at[side], small_s.at[j], small_r.at[j], (right, left)[side])
-             for j, (src, dst) in enumerate([(wind, wind_h), (land, land_h)]) for side in range(2)]
-    energy_msg = [[remote(e_send.at[s], e_halo.at[s, side], e_s.at[s], e_r.at[s],
-                          (right, left)[side]) for side in range(2)] for s in range(2)]
+    ends = (pl.ds(SUB - 2, 2), pl.ds(0, 2))
+    small = [remote(src, dst, small_s.at[j], small_r.at[j], (right, left)[side])
+             for side in range(2) for j, (src, dst) in enumerate([
+                 (wind.at[:, ends[side]], wind_h.at[side, :, ends[side]]),
+                 (land.at[ends[side]], land_h.at[side, ends[side]])])]
+    energy_msg = [[remote(e_send.at[s, ends[side]], e_halo.at[s, side, ends[side]], e_s.at[s],
+                          e_r.at[s], (right, left)[side]) for side in range(2)] for s in range(2)]
+    wind_rows, land_rows = wind_h.at[:, :, ends[1]], land_h.at[:, ends[1]]
 
     columns_here(0)
     pl.semaphore_wait(barrier, 2)
@@ -232,30 +236,50 @@
 
             over_tiles(body, 0, 6)
 
-    def fix(step, sums):
+    def contribute(acc, d, moved, grown):
+        cosine, sine = scalars(d)
+        acc = list(acc)
+        flux = zero
+        for f in range(groups):
+            flux = flux + freq[3, f] * (grown[f] - moved[f])
+            acc[2 + f] = acc[2 + f] + cosine * grown[f]
+            acc[2 + groups + f] = acc[2 + groups + f] + sine * grown[f]
+        acc[0] = acc[0] + cosine * flux
+        acc[1] = acc[1] + sine * flux
+        return acc
+
+    def fix(step, sums, parts=None):
         totals = {}
         for side, d0, skip, east, slot, edge in edges():
-            def body(i, total, d0=d0, skip=skip, east=east, side=side, slot=slot, edge=edge):
+            def body(i, carry, d0=d0, skip=skip, side=side, slot=slot, edge=edge):
+                total, acc = carry[0], carry[1:]
                 d = d0 + i + skip * (i // quarter)
+                moved, grown = [], []
                 for f in range(groups):
                     at = pl.ds((i * groups + f) * SUB, SUB)
-                    along_x = table[1, d * groups + f]
+                    cell = (d * groups + f) * SUB + edge
                     if step == 0:
-                        extra = along_x * halo[0, side, at, :]
+                        extra = table[1, d * groups + f] * halo[0, side, at, :]
                     else:
-                        flow = r_ref[slot + 4 * (step - 1), f] * (
+                        extra = r_ref[slot + 4 * (step - 1), f] * (
                             halo[0, side, at, :] + coef[side, at, :] * halo[step, side, at, :])
                         if step == 1:
-                            halo[0, side, at, :] = flow
-                            extra = along_x * flow
-                        else:
-                            extra = flow
-                    cell = (d * groups + f) * SUB + edge
+                            halo[0, side, at, :] = extra
+                            extra = table[1, d * groups + f] * extra
                     w_ref[cell] = w_ref[cell] + extra
                     total = total + extra
-                return total
-
-            totals[edge] = over_tiles(body, sums[edge], 6)
+                    moved.append(extra)
+                    if acc:
+                        grown.append(g_ref[cell] * extra)
+                if acc:
+                    acc = contribute(acc, d, moved, grown)
+                return (total, *acc)
+
+            start = (sums[edge],) + (tuple(parts[edge]) if parts else ())
+            done = over_tiles(body, start, 6)
+            totals[edge] = done[0]
+            if parts:
+                parts[edge] = done[1:]
         return tuple(totals.get(x, sums[x]) for x in range(SUB))
 
     def energy_rows(sums, which):
@@ -276,14 +300,43 @@
 
     inner, outer = list(range(1, SUB - 1)), [0, SUB - 1]
 
-    def gathered(which, sums):
+    def last_factors(which, sums):
         for x, row in zip(which, energy_rows(sums, which)):
             tile = row * (1.0 / cells)
             ratio = jnp.broadcast_to(tile / (0.5 + tile), (SUB, 128))
             for f in range(groups):
-                value = mask_b[x] / (1.0 + freq[2, f] * ratio)
-                r_ref[x, f] = value
-                drift_ref[x, f] = freq[3, f] * value
+                r_ref[x, f] = mask_b[x] / (1.0 + freq[2, f] * ratio)
+
+    def row_sums(which, values):
+        rows_of = {}
+        for c in range(4):
+            for j, x in enumerate(which):
+                value = values[c * len(which) + j]
+                if c < 2:
+                    value = value * mask_b[x]
+                rows_of[c * SUB + x] = jnp.sum(value, axis=0, keepdims=True)
+        return rows_of
+
+    def gathered_outer():
+        size = 2 + 2 * groups
+
+        def gather(d, carry):
+            done = []
+            for j, x in enumerate(outer):
+                cells_of = [(d * groups + f) * SUB + x for f in range(groups)]
+                moved = [w_ref[at] for at in cells_of]
+                grown = [g_ref[at] * value for at, value in zip(cells_of, moved)]
+                done += contribute(carry[j * size:(j + 1) * size], d, moved, grown)
+            return tuple(done)
+
+        total = lax.fori_loop(0, dirs, gather, (zero,) * (2 * size), unroll=2)
+        return {x: total[j * size:(j + 1) * size] for j, x in enumerate(outer)}
+
+    def gathered(which, sums):
+        last_factors(which, sums)
+        for x in which:
+            for f in range(groups):
+                drift_ref[x, f] = freq[3, f] * r_ref[x, f]
 
         def gather(d, carry):
             cosine, sine = scalars(d)
@@ -303,12 +356,13 @@
                 carry[3 * m + j] = carry[3 * m + j] + sine * drift
             return tuple(carry)
 
-        return lax.fori_loop(0, dirs, gather, (zero,) * (4 * len(which)), unroll=2)
+        return row_sums(which, lax.fori_loop(
+            0, dirs, gather, (zero,) * (4 * len(which)), unroll=2))
 
     sums = main(0, (zero,) * SUB)
     spread_word(range(0, 1) if reaches else [])
-    arrived(wind_h, small_r.at[0])
-    arrived(land_h, small_r.at[1])
+    arrived(wind_rows, small_r.at[0])
+    arrived(land_rows, small_r.at[1])
     for side in range(2):
         tiles = [wind_h[side, 0], wind_h[side, 1]]
         land_tile = land_h[side]
@@ -318,6 +372,7 @@
     grow_halo()
     arrived(halo.at[0], bulk_r.at[0])
     sums = fix(0, sums)
+    outer_parts = None
     for step in (1, 2):
         tile = energy_tile(sums)
         e_send[step - 1] = tile
@@ -332,9 +387,10 @@
             spread_word(range(2, len(reaches)))
         prepare(step)
         if step == 2:
-            inner_sums = gathered(inner, sums)
+            inner_rows = gathered(inner, sums)
+            outer_parts = gathered_outer()
         arrived(halo.at[step], bulk_r.at[step])
-        arrived(e_halo.at[step - 1], e_r.at[step - 1])
+        arrived(e_halo.at[step - 1, :, ends[1]], e_r.at[step - 1])
         for side in range(2):
             seen = e_halo[step - 1, side]
             ratio = seen / (0.5 + seen)
@@ -342,21 +398,20 @@
             for depth in range(3 - step):
                 factor(ratio, SUB - 1 - depth if side == 0 else depth, base + depth,
                        base + depth + 4 * (step - 1))
-        sums = fix(step, sums)
-
-    outer_sums = gathered(outer, sums)
-    both = {}
-    for which, parts in ((inner, inner_sums), (outer, outer_sums)):
-        for c in range(4):
-            for j, x in enumerate(which):
-                both[c * SUB + x] = parts[c * len(which) + j]
-    carry = [both[j] for j in range(4 * SUB)]
-
-    total = []
-    for j, value in enumerate(carry):
-        if j < 2 * SUB:
-            value = value * mask_b[j % SUB]
-        total.append(jnp.sum(value, axis=0, keepdims=True))
+        sums = fix(step, sums, outer_parts)
+
+    last_factors(outer, sums)
+    values = [None] * 8
+    for j, x in enumerate(outer):
+        part = outer_parts[x]
+        values[j], values[2 + j] = part[0], part[1]
+        for c in range(2):
+            drift = zero
+            for f in range(groups):
+                drift = drift + (freq[3, f] * r_ref[x, f]) * part[2 + c * groups + f]
+            values[4 + 2 * c + j] = drift
+    all_rows = {**inner_rows, **row_sums(outer, values)}
+    total = [all_rows[j] for j in range(4 * SUB)]
     total.append(jnp.zeros((128 - 4 * SUB, 128), jnp.float32))
     stacked = jnp.concatenate(total, axis=0)
     lat = lax.broadcasted_iota(jnp.int32, (128, 128), 0)
@@ -387,10 +442,10 @@
 
     lax.fori_loop(0, dirs, write, 0, unroll=2)
     arrived(send, bulk_s.at[0])
-    arrived(wind_h, small_s.at[0])
-    arrived(land_h, small_s.at[1])
+    arrived(wind_rows, small_s.at[0])
+    arrived(land_rows, small_s.at[1])
     for s in range(2):
-        arrived(e_halo.at[s], e_s.at[s])
+        arrived(e_halo.at[s, :, ends[1]], e_s.at[s])
     others = sends.at[pl.ds(0, n - 1)]
     arrived(others, a_s.at[0])
     arrived(others, a_r.at[0])

time: 34.4 us -> 33.7 us (0.980)
  Pallas kernels: 33.6 us -> 32.9 us
    pallas_call x1, Pallas kernels: 31.4 us -> 30.7 us  [per_device(): pl.pallas_call(functools.partial(kernel, n, dirs, groups), out_shape=(plt...]
where the time goes in v3:
time: 33.7 us; the launch traced here: 33.6 us
  Pallas kernels  32.9 us (98%)
  between operations  0.64 us (2%)
    pallas_call x1, Pallas kernels, per_device(): pl.pallas_call(functools.partial(kernel, n, dirs, groups), out_shape=(plt...  30.7 us
    pallas_call x1, Pallas kernels, per_device(): pl.pallas_call(functools.partial(finish_kernel, n, parts), out_shape=(jax...  2.25 us

profile of v3, /device:TPU:0, one launch (start us, length us, event | category | flops | bytes accessed | tf_op | source)
XLA Modules:
  0.0 33.6 jit_solution(15583309015734242204)
XLA Ops:
  0.6 30.7 %wave_window.1 = (f32[9216,128]{1,0:T(8,128)S(1)}, f32[16,8,128]{2,1,0:T(8,128)S(1)}) custom-call(f32[1152,8,128]{2,1,0:T(8,128)} %bitcast.3, f32[2,8,128]{2,1,0:T(8,128)} %wind_in.1, s32[8,128]{1,0:T(8,128)} %land_in.1, s32[1,128]{1,0:T(1,128)} %bitcast.4), custom_call_target="tpu_custom_call" | custom-call | tf_op jit(solution)/shard_map/wave_window/pallas_call | solution.py:486
  31.3 2.3 %hand_over.1 = (f32[9216,128]{1,0:T(8,128)}, f32[4,8,128]{2,1,0:T(8,128)}) custom-call(f32[9216,128]{1,0:T(8,128)S(1)} %get-tuple-element.6.out, f32[16,8,128]{2,1,0:T(8,128)S(1)} %get-tuple-element.7.recv), custom_call_target="tpu_custom_call" | custom-call | tf_op jit(solution)/shard_map/hand_over/pallas_call | solution.py:534

commit v4 on v3

--- a/solution.py
+++ b/solution.py
@@ -15,7 +15,7 @@
 
 def kernel(n, dirs, groups, spec, wind_in, land_in, bands_in, out, recv,
            trig, freq, wind, land, bands, x_ref, w_ref, g_ref, send, halo, wind_h, land_h,
-           wind_b, mask_b, r_ref, drift_ref, e_send, e_halo, rows, sends, coef, table, grow_h,
+           wind_b, mask_b, r_ref, drift_ref, e_send, e_halo, pick_t, sends, coef, table, grow_h,
            in_sem, small_sem, col_sem, meet, bulk_s, bulk_r, small_s, small_r, e_s, e_r, a_s, a_r):
     me = lax.axis_index("gx")
     right, left = lax.rem(me + 1, n), lax.rem(me + n - 1, n)
@@ -37,23 +37,28 @@
 
     in_copy = pltpu.make_async_copy(spec, x_ref, in_sem.at[0])
 
-    def column_copies(k):
+    def column_copies(k, side):
+        column = k if side else SUB - 1 - k
         return [pltpu.make_async_copy(
-            spec.at[pl.ds(first, bins), column], send.at[k, side, pl.ds(to, bins)], col_sem.at[k])
-            for first, bins, side, to, column in [
-                (0, qbins, 0, 0, SUB - 1 - k), (3 * qbins, qbins, 0, qbins, SUB - 1 - k),
-                (qbins, 2 * qbins, 1, 0, k)]]
-
-    def columns_here(k):
-        pltpu.make_async_copy(send.at[k], halo.at[k], col_sem.at[k]).wait()
+            spec.at[pl.ds(first * qbins, qbins), column],
+            send.at[k, side, pl.ds(j * qbins, qbins)], col_sem.at[2 * k + side])
+            for j, first in enumerate([(0, 3), (1, 2)][side])]
+
+    def column_here(k, side):
+        pltpu.make_async_copy(send.at[k, side], halo.at[k, side], col_sem.at[2 * k + side]).wait()
 
     tables_in = [pltpu.make_async_copy(src, dst, small_sem.at[i]) for i, (src, dst) in enumerate(
         [(wind_in, wind), (land_in, land), (bands_in, bands)])]
-    columns_in = [column_copies(k) for k in range(3)]
-    for copy in columns_in[0] + tables_in:
-        copy.start()
+    columns_in = [[column_copies(k, side) for side in range(2)] for k in range(3)]
+    odd = lax.rem(me, 2)
+    for parity in range(2):
+        @pl.when(odd == parity)
+        def _(parity=parity):
+            for copy in tables_in[:2] + columns_in[0][1 - parity] + columns_in[0][parity]:
+                copy.start()
+    tables_in[2].start()
     in_copy.start()
-    for copy in columns_in[1] + columns_in[2]:
+    for copy in sum(columns_in[1] + columns_in[2], []):
         copy.start()
 
     for d in range(dirs):
@@ -78,7 +83,8 @@
     def arrived(ref, sem):
         pltpu.make_async_copy(ref, ref, sem).wait()
 
-    bulk = [[remote(send.at[k, side], halo.at[k, side], bulk_s.at[0], bulk_r.at[k],
+    bulk = [[remote(send.at[k, side], halo.at[k, side], bulk_s.at[0],
+                    bulk_r.at[k + side * (k // 2)],
                     (right, left)[side]) for side in range(2)] for k in range(3)]
     ends = (pl.ds(SUB - 2, 2), pl.ds(0, 2))
     small = [remote(src, dst, small_s.at[j], small_r.at[j], (right, left)[side])
@@ -86,15 +92,23 @@
                  (wind.at[:, ends[side]], wind_h.at[side, :, ends[side]]),
                  (land.at[ends[side]], land_h.at[side, ends[side]])])]
     energy_msg = [[remote(e_send.at[s, ends[side]], e_halo.at[s, side, ends[side]], e_s.at[s],
-                          e_r.at[s], (right, left)[side]) for side in range(2)] for s in range(2)]
+                          e_r.at[s + side * s], (right, left)[side]) for side in range(2)] for s in range(2)]
     wind_rows, land_rows = wind_h.at[:, :, ends[1]], land_h.at[:, ends[1]]
 
-    columns_here(0)
+    column_here(0, 1 - odd)
     pl.semaphore_wait(barrier, 2)
     for copy in tables_in:
         copy.wait()
-    for copy in small + bulk[0]:
+    for copy in small:
         copy.start()
+
+    def first_column(side):
+        remote(send.at[0, side], halo.at[0, side], bulk_s.at[0], bulk_r.at[0],
+               jnp.where(side == 0, right, left)).start()
+
+    first_column(1 - odd)
+    column_here(0, odd)
+    first_column(odd)
     if reaches:
         greet(meet.at[0], reaches[0])
 
@@ -109,8 +123,9 @@
     for x in range(SUB):
         spread(x, own_wind, own_land, x)
 
-    columns_here(1)
-    columns_here(2)
+    for k in (1, 2):
+        for side in range(2):
+            column_here(k, side)
 
     def launch(k, when):
         @pl.when(when)
@@ -248,38 +263,24 @@
         acc[1] = acc[1] + sine * flux
         return acc
 
-    def fix(step, sums, parts=None):
+    def fix(step, sums):
         totals = {}
         for side, d0, skip, east, slot, edge in edges():
-            def body(i, carry, d0=d0, skip=skip, side=side, slot=slot, edge=edge):
-                total, acc = carry[0], carry[1:]
+            def body(i, total, d0=d0, skip=skip, side=side, slot=slot, edge=edge):
                 d = d0 + i + skip * (i // quarter)
-                moved, grown = [], []
                 for f in range(groups):
                     at = pl.ds((i * groups + f) * SUB, SUB)
+                    flow = halo[0, side, at, :]
+                    if step == 1:
+                        flow = r_ref[slot, f] * (flow + coef[side, at, :] * halo[1, side, at, :])
+                        halo[0, side, at, :] = flow
+                    extra = table[1, d * groups + f] * flow
                     cell = (d * groups + f) * SUB + edge
-                    if step == 0:
-                        extra = table[1, d * groups + f] * halo[0, side, at, :]
-                    else:
-                        extra = r_ref[slot + 4 * (step - 1), f] * (
-                            halo[0, side, at, :] + coef[side, at, :] * halo[step, side, at, :])
-                        if step == 1:
-                            halo[0, side, at, :] = extra
-                            extra = table[1, d * groups + f] * extra
                     w_ref[cell] = w_ref[cell] + extra
                     total = total + extra
-                    moved.append(extra)
-                    if acc:
-                        grown.append(g_ref[cell] * extra)
-                if acc:
-                    acc = contribute(acc, d, moved, grown)
-                return (total, *acc)
-
-            start = (sums[edge],) + (tuple(parts[edge]) if parts else ())
-            done = over_tiles(body, start, 6)
-            totals[edge] = done[0]
-            if parts:
-                parts[edge] = done[1:]
+                return total
+
+            totals[edge] = over_tiles(body, sums[edge], 6)
         return tuple(totals.get(x, sums[x]) for x in range(SUB))
 
     def energy_rows(sums, which):
@@ -359,6 +360,8 @@
         return row_sums(which, lax.fori_loop(
             0, dirs, gather, (zero,) * (4 * len(which)), unroll=2))
 
+    lat = lax.broadcasted_iota(jnp.int32, (128, 128), 0)
+    pick_t[...] = (lat == bands[...]).astype(jnp.float32).T
     sums = main(0, (zero,) * SUB)
     spread_word(range(0, 1) if reaches else [])
     arrived(wind_rows, small_r.at[0])
@@ -372,7 +375,6 @@
     grow_halo()
     arrived(halo.at[0], bulk_r.at[0])
     sums = fix(0, sums)
-    outer_parts = None
     for step in (1, 2):
         tile = energy_tile(sums)
         e_send[step - 1] = tile
@@ -389,16 +391,55 @@
         if step == 2:
             inner_rows = gathered(inner, sums)
             outer_parts = gathered_outer()
-        arrived(halo.at[step], bulk_r.at[step])
-        arrived(e_halo.at[step - 1, :, ends[1]], e_r.at[step - 1])
+        if step == 2:
+            break
+        arrived(halo.at[1], bulk_r.at[1])
+        arrived(e_halo.at[0, :, ends[1]], e_r.at[0])
         for side in range(2):
-            seen = e_halo[step - 1, side]
+            seen = e_halo[0, side]
             ratio = seen / (0.5 + seen)
             base = LEFT if side == 0 else RIGHT
-            for depth in range(3 - step):
-                factor(ratio, SUB - 1 - depth if side == 0 else depth, base + depth,
-                       base + depth + 4 * (step - 1))
-        sums = fix(step, sums, outer_parts)
+            for depth in range(2):
+                factor(ratio, SUB - 1 - depth if side == 0 else depth, base + depth, base + depth)
+        sums = fix(1, sums)
+
+    def by_side(first, second):
+        return [jnp.where(odd == 1, a, b) for a, b in zip(first, second)]
+
+    def last_fix(side, start):
+        arrived(halo.at[2, side], bulk_r.at[2 + side])
+        arrived(e_halo.at[1, side, ends[1]], e_r.at[1 + side])
+        slot, edge = LEFT + side * (RIGHT - LEFT), side * (SUB - 1)
+        seen = e_halo[1, side, pl.ds((1 - side) * (SUB - 1), 1), :]
+        ratio = jnp.broadcast_to(seen / (0.5 + seen), (SUB, 128))
+        scale = [mask_b[slot] / (1.0 + freq[2, f] * ratio) for f in range(groups)]
+        for f in range(groups):
+            r_ref[slot + 4, f] = scale[f]
+
+        def body(i, carry):
+            total, acc = carry[0], carry[1:]
+            d = side * quarter + i + (1 - side) * 2 * quarter * (i // quarter)
+            moved, grown = [], []
+            for f in range(groups):
+                at = pl.ds((i * groups + f) * SUB, SUB)
+                cell = (d * groups + f) * SUB + edge
+                extra = r_ref[slot + 4, f] * (
+                    halo[0, side, at, :] + coef[side, at, :] * halo[2, side, at, :])
+                w_ref[cell] = w_ref[cell] + extra
+                total = total + extra
+                moved.append(extra)
+                grown.append(g_ref[cell] * extra)
+            return (total, *contribute(acc, d, moved, grown))
+
+        return over_tiles(body, tuple(start), 6)
+
+    west_edge = (sums[0], *outer_parts[0])
+    east_edge = (sums[SUB - 1], *outer_parts[SUB - 1])
+    near = last_fix(1 - odd, by_side(west_edge, east_edge))
+    far = last_fix(odd, by_side(east_edge, west_edge))
+    west_edge, east_edge = by_side(near, far), by_side(far, near)
+    sums = (west_edge[0],) + tuple(sums[1:-1]) + (east_edge[0],)
+    outer_parts = {0: west_edge[1:], SUB - 1: east_edge[1:]}
 
     last_factors(outer, sums)
     values = [None] * 8
@@ -414,21 +455,20 @@
     total = [all_rows[j] for j in range(4 * SUB)]
     total.append(jnp.zeros((128 - 4 * SUB, 128), jnp.float32))
     stacked = jnp.concatenate(total, axis=0)
-    lat = lax.broadcasted_iota(jnp.int32, (128, 128), 0)
-    pick = (lat == bands[...]).astype(jnp.float32)
-    picked = jnp.dot(stacked, pick, precision=lax.Precision.HIGHEST,
-                     preferred_element_type=jnp.float32)
-    rows[...] = picked.T
+    picked = lax.dot_general(
+        pick_t[...], stacked, (((1,), (1,)), ((), ())), precision=lax.Precision.HIGHEST,
+        preferred_element_type=jnp.float32)
     band = 128 // n
     for k in range(n):
-        sends[k] = rows[pl.ds(k * band, band), :]
+        sends[k] = picked[k * band:(k + 1) * band]
 
     def begin(i, _):
-        target = lax.rem(me + i, n)
+        step = (i // 2) * (1 - 2 * lax.rem(i, 2))
+        target = lax.rem(me + n // 2 + step + n, n)
         remote(sends.at[target], recv.at[me], a_s.at[0], a_r.at[0], target).start()
         return 0
 
-    lax.fori_loop(1, n, begin, 0)
+    lax.fori_loop(1, n, begin, 0, unroll=3)
     recv[pl.ds(me, 1)] = sends[pl.ds(me, 1)]
 
     def write(d, _):
@@ -514,14 +554,14 @@
             pltpu.VMEM((2, 2, half, lats), f32),
             pltpu.SemaphoreType.DMA((1,)),
             pltpu.SemaphoreType.DMA((3,)),
-            pltpu.SemaphoreType.DMA((3,)),
+            pltpu.SemaphoreType.DMA((6,)),
             pltpu.SemaphoreType.REGULAR((max(1, (n // 2 - 1).bit_length()),)),
             pltpu.SemaphoreType.DMA((1,)),
-            pltpu.SemaphoreType.DMA((3,)),
+            pltpu.SemaphoreType.DMA((4,)),
             pltpu.SemaphoreType.DMA((2,)),
             pltpu.SemaphoreType.DMA((2,)),
             pltpu.SemaphoreType.DMA((2,)),
-            pltpu.SemaphoreType.DMA((2,)),
+            pltpu.SemaphoreType.DMA((3,)),
             pltpu.SemaphoreType.DMA((1,)),
             pltpu.SemaphoreType.DMA((1,)),
         ],
@@ -530,7 +570,7 @@
         name="wave_window",
     )(*[pltpu.with_memory_space_constraint(a, pltpu.HBM) for a in (
         spectrum.reshape(cells, SUB, lats), wind, land_sea, band_rows.reshape(1, lats))])
-    parts = 4
+    parts = 1
     after, ocean = pl.pallas_call(
         functools.partial(finish_kernel, n, parts),
         out_shape=(jax.ShapeDtypeStruct((cells * SUB, lats), f32),

time: 33.7 us -> 34 us (level)
  no operation moved by 1% of the time
where the time goes in v4:
time: 34 us; the launch traced here: 33.9 us
  Pallas kernels  33.2 us (98%)
  between operations  0.64 us (2%)
    pallas_call x1, Pallas kernels, per_device(): pl.pallas_call(functools.partial(kernel, n, dirs, groups), out_shape=(plt...  31 us
    pallas_call x1, Pallas kernels, per_device(): pl.pallas_call(functools.partial(finish_kernel, n, parts), out_shape=(jax...  2.23 us

profile of v4, /device:TPU:0, one launch (start us, length us, event | category | flops | bytes accessed | tf_op | source)
XLA Modules:
  0.0 33.9 jit_solution(1228876395327928705)
XLA Ops:
  0.6 31.0 %wave_window.1 = (f32[9216,128]{1,0:T(8,128)S(1)}, f32[16,8,128]{2,1,0:T(8,128)S(1)}) custom-call(f32[1152,8,128]{2,1,0:T(8,128)} %bitcast.3, f32[2,8,128]{2,1,0:T(8,128)} %wind_in.1, s32[8,128]{1,0:T(8,128)} %land_in.1, s32[1,128]{1,0:T(1,128)} %bitcast.4), custom_call_target="tpu_custom_call" | custom-call | tf_op jit(solution)/shard_map/wave_window/pallas_call | solution.py:526
  31.6 2.2 %hand_over.1 = (f32[9216,128]{1,0:T(8,128)}, f32[4,8,128]{2,1,0:T(8,128)}) custom-call(f32[9216,128]{1,0:T(8,128)S(1)} %get-tuple-element.6.out, f32[16,8,128]{2,1,0:T(8,128)S(1)} %get-tuple-element.7.recv), custom_call_target="tpu_custom_call" | custom-call | tf_op jit(solution)/shard_map/hand_over/pallas_call | solution.py:574

commit v5 on v4

--- a/solution.py
+++ b/solution.py
@@ -11,6 +11,11 @@
 STEPS = 3
 SUB = 8
 LEFT, RIGHT = 8, 10
+
+
+def packing(n):
+    pack = min(4, 128 // n)
+    return pack, 128 // pack
 
 
 def kernel(n, dirs, groups, spec, wind_in, land_in, bands_in, out, recv,
@@ -37,28 +42,23 @@
 
     in_copy = pltpu.make_async_copy(spec, x_ref, in_sem.at[0])
 
-    def column_copies(k, side):
-        column = k if side else SUB - 1 - k
+    def column_copies(k):
         return [pltpu.make_async_copy(
-            spec.at[pl.ds(first * qbins, qbins), column],
-            send.at[k, side, pl.ds(j * qbins, qbins)], col_sem.at[2 * k + side])
-            for j, first in enumerate([(0, 3), (1, 2)][side])]
-
-    def column_here(k, side):
-        pltpu.make_async_copy(send.at[k, side], halo.at[k, side], col_sem.at[2 * k + side]).wait()
+            spec.at[pl.ds(first, bins), column], send.at[k, side, pl.ds(to, bins)], col_sem.at[k])
+            for first, bins, side, to, column in [
+                (0, qbins, 0, 0, SUB - 1 - k), (3 * qbins, qbins, 0, qbins, SUB - 1 - k),
+                (qbins, 2 * qbins, 1, 0, k)]]
+
+    def columns_here(k):
+        pltpu.make_async_copy(send.at[k], halo.at[k], col_sem.at[k]).wait()
 
     tables_in = [pltpu.make_async_copy(src, dst, small_sem.at[i]) for i, (src, dst) in enumerate(
         [(wind_in, wind), (land_in, land), (bands_in, bands)])]
-    columns_in = [[column_copies(k, side) for side in range(2)] for k in range(3)]
-    odd = lax.rem(me, 2)
-    for parity in range(2):
-        @pl.when(odd == parity)
-        def _(parity=parity):
-            for copy in tables_in[:2] + columns_in[0][1 - parity] + columns_in[0][parity]:
-                copy.start()
-    tables_in[2].start()
+    columns_in = [column_copies(k) for k in range(3)]
+    for copy in columns_in[0] + tables_in:
+        copy.start()
     in_copy.start()
-    for copy in sum(columns_in[1] + columns_in[2], []):
+    for copy in columns_in[1] + columns_in[2]:
         copy.start()
 
     for d in range(dirs):
@@ -95,20 +95,12 @@
                           e_r.at[s + side * s], (right, left)[side]) for side in range(2)] for s in range(2)]
     wind_rows, land_rows = wind_h.at[:, :, ends[1]], land_h.at[:, ends[1]]
 
-    column_here(0, 1 - odd)
+    columns_here(0)
     pl.semaphore_wait(barrier, 2)
     for copy in tables_in:
         copy.wait()
-    for copy in small:
+    for copy in small + bulk[0]:
         copy.start()
-
-    def first_column(side):
-        remote(send.at[0, side], halo.at[0, side], bulk_s.at[0], bulk_r.at[0],
-               jnp.where(side == 0, right, left)).start()
-
-    first_column(1 - odd)
-    column_here(0, odd)
-    first_column(odd)
     if reaches:
         greet(meet.at[0], reaches[0])
 
@@ -123,9 +115,8 @@
     for x in range(SUB):
         spread(x, own_wind, own_land, x)
 
-    for k in (1, 2):
-        for side in range(2):
-            column_here(k, side)
+    columns_here(1)
+    columns_here(2)
 
     def launch(k, when):
         @pl.when(when)
@@ -403,6 +394,8 @@
                 factor(ratio, SUB - 1 - depth if side == 0 else depth, base + depth, base + depth)
         sums = fix(1, sums)
 
+    odd = lax.rem(me, 2)
+
     def by_side(first, second):
         return [jnp.where(odd == 1, a, b) for a, b in zip(first, second)]
 
@@ -453,14 +446,25 @@
             values[4 + 2 * c + j] = drift
     all_rows = {**inner_rows, **row_sums(outer, values)}
     total = [all_rows[j] for j in range(4 * SUB)]
-    total.append(jnp.zeros((128 - 4 * SUB, 128), jnp.float32))
-    stacked = jnp.concatenate(total, axis=0)
+    pack, width = packing(n)
+    if width > 4 * SUB:
+        total.append(jnp.zeros((width - 4 * SUB, 128), jnp.float32))
+    stacked = jnp.concatenate(total * pack, axis=0)
     picked = lax.dot_general(
         pick_t[...], stacked, (((1,), (1,)), ((), ())), precision=lax.Precision.HIGHEST,
         preferred_element_type=jnp.float32)
-    band = 128 // n
-    for k in range(n):
-        sends[k] = picked[k * band:(k + 1) * band]
+    row = lax.broadcasted_iota(jnp.int32, (SUB, 128), 0)
+    mine = lax.rem(row, pack) == lane // width
+    lines = 128 // n // pack
+    for m in range(128 // SUB):
+        tile = jnp.where(mine, picked[m * SUB:(m + 1) * SUB], 0.0)
+        shift = 1
+        while shift < pack:
+            tile = tile + pltpu.roll(tile, SUB - shift, 0)
+            shift *= 2
+        for q in range(SUB // pack):
+            k, line = divmod(m * (SUB // pack) + q, lines)
+            sends[k, line:line + 1, :] = tile[q * pack:q * pack + 1]
 
     def begin(i, _):
         step = (i // 2) * (1 - 2 * lax.rem(i, 2))
@@ -501,11 +505,22 @@
     band = 128 // n
     per_tile = 128 // SUB
     block = lax.broadcasted_iota(jnp.int32, (band, 128), 1) // SUB
+    pack, width = packing(n)
+    place = lax.rem(lax.broadcasted_iota(jnp.int32, (band, 128), 0), pack)
+    unpacked = []
+    for k in range(n):
+        lines = recv[k]
+        spread = jnp.concatenate(
+            [jnp.broadcast_to(lines[q:q + 1], (pack, 128)) for q in range(band // pack)], axis=0)
+        value = spread
+        for j in range(1, pack):
+            value = jnp.where(place == j, pltpu.roll(spread, 128 - j * width, 1), value)
+        unpacked.append(value)
     for tile in range(max(1, n // per_tile)):
         for c in range(4):
             built = jnp.zeros((band, 128), jnp.float32)
             for k in range(min(n, per_tile)):
-                moved = pltpu.roll(recv[tile * per_tile + k], (SUB * (k - c)) % 128, 1)
+                moved = pltpu.roll(unpacked[tile * per_tile + k], (SUB * (k - c)) % 128, 1)
                 built = jnp.where(block == k, moved, built)
             ocean[c, :, tile * 128:(tile + 1) * 128] = built
     copies.append(pltpu.make_async_copy(ocean, ocean_out, sem.at[parts]))
@@ -525,7 +540,7 @@
     cells = dirs * groups * SUB
     after, recv = pl.pallas_call(
         functools.partial(kernel, n, dirs, groups),
-        out_shape=(pltpu.VMEM((cells * SUB, lats), f32), pltpu.VMEM((n, band, 128), f32)),
+        out_shape=(pltpu.VMEM((cells * SUB, lats), f32), pltpu.VMEM((n, band // packing(n)[0], 128), f32)),
         in_specs=[anywhere] * 4,
         out_specs=(vmem, vmem),
         scratch_shapes=[
@@ -548,13 +563,13 @@
             pltpu.VMEM((2, SUB, lats), f32),
             pltpu.VMEM((2, 2, SUB, lats), f32),
             pltpu.VMEM((128, 128), f32),
-            pltpu.VMEM((n, band, 128), f32),
+            pltpu.VMEM((n, band // packing(n)[0], 128), f32),
             pltpu.VMEM((2, half, lats), f32),
             pltpu.VMEM((3, dirs * groups, SUB, lats), f32),
             pltpu.VMEM((2, 2, half, lats), f32),
             pltpu.SemaphoreType.DMA((1,)),
             pltpu.SemaphoreType.DMA((3,)),
-            pltpu.SemaphoreType.DMA((6,)),
+            pltpu.SemaphoreType.DMA((3,)),
             pltpu.SemaphoreType.REGULAR((max(1, (n // 2 - 1).bit_length()),)),
             pltpu.SemaphoreType.DMA((1,)),
             pltpu.SemaphoreType.DMA((4,)),

time: 34 us -> 33.7 us (level)
  no operation moved by 1% of the time
where the time goes in v5:
time: 33.7 us; the launch traced here: 33.6 us
  Pallas kernels  32.9 us (98%)
  between operations  0.64 us (2%)
    pallas_call x1, Pallas kernels, per_device(): pl.pallas_call(functools.partial(kernel, n, dirs, groups), out_shape=(plt...  30.7 us
    pallas_call x1, Pallas kernels, per_device(): pl.pallas_call(functools.partial(finish_kernel, n, parts), out_shape=(jax...  2.21 us

profile of v5, /device:TPU:0, one launch (start us, length us, event | category | flops | bytes accessed | tf_op | source)
XLA Modules:
  0.0 33.6 jit_solution(3625492455099473162)
XLA Ops:
  0.6 30.7 %wave_window.1 = (f32[9216,128]{1,0:T(8,128)S(1)}, f32[16,2,128]{2,1,0:T(2,128)S(1)}) custom-call(f32[1152,8,128]{2,1,0:T(8,128)} %bitcast.3, f32[2,8,128]{2,1,0:T(8,128)} %wind_in.1, s32[8,128]{1,0:T(8,128)} %land_in.1, s32[1,128]{1,0:T(1,128)} %bitcast.4), custom_call_target="tpu_custom_call" | custom-call | tf_op jit(solution)/shard_map/wave_window/pallas_call | solution.py:541
  31.3 2.2 %hand_over.1 = (f32[9216,128]{1,0:T(8,128)}, f32[4,8,128]{2,1,0:T(8,128)}) custom-call(f32[9216,128]{1,0:T(8,128)S(1)} %get-tuple-element.6.out, f32[16,2,128]{2,1,0:T(2,128)S(1)} %get-tuple-element.7.recv), custom_call_target="tpu_custom_call" | custom-call | tf_op jit(solution)/shard_map/hand_over/pallas_call | solution.py:589

commit v6 on v5

--- a/solution.py
+++ b/solution.py
@@ -130,8 +130,9 @@
             if i + 1 < len(reaches):
                 greet(meet.at[i + 1], reaches[i + 1])
 
-    for copy in bulk[1]:
-        copy.start()
+    inner_late = jnp.logical_and(late, jnp.logical_and(lax.rem(me, 2) == 1, me != n - 1))
+    first_late = me == 0
+    launch(1, jnp.logical_not(jnp.logical_or(inner_late, first_late)))
     in_copy.wait()
 
     def scalars(d):
@@ -372,13 +373,18 @@
         own_factors(tile)
         for copy in energy_msg[step - 1]:
             copy.start()
+        if step == 1:
+            launch(1, first_late)
         launch(2, late if step == 2 else jnp.logical_not(late))
         sums = main(step, (zero,) * SUB)
         if step == 1:
+            launch(1, inner_late)
             spread_word(range(1, min(2, len(reaches))))
         else:
             spread_word(range(2, len(reaches)))
         prepare(step)
+        if step == 1:
+            pass
         if step == 2:
             inner_rows = gathered(inner, sums)
             outer_parts = gathered_outer()

time: 33.7 us -> 33.7 us (level)
  no operation moved by 1% of the time
where the time goes in v6:
time: 33.7 us; the launch traced here: 33.5 us
  Pallas kernels  32.9 us (98%)
  between operations  0.64 us (2%)
    pallas_call x1, Pallas kernels, per_device(): pl.pallas_call(functools.partial(kernel, n, dirs, groups), out_shape=(plt...  30.7 us
    pallas_call x1, Pallas kernels, per_device(): pl.pallas_call(functools.partial(finish_kernel, n, parts), out_shape=(jax...  2.21 us

profile of v6, /device:TPU:0, one launch (start us, length us, event | category | flops | bytes accessed | tf_op | source)
XLA Modules:
  0.0 33.5 jit_solution(7954520797835490348)
XLA Ops:
  0.6 30.7 %wave_window.1 = (f32[9216,128]{1,0:T(8,128)S(1)}, f32[16,2,128]{2,1,0:T(2,128)S(1)}) custom-call(f32[1152,8,128]{2,1,0:T(8,128)} %bitcast.3, f32[2,8,128]{2,1,0:T(8,128)} %wind_in.1, s32[8,128]{1,0:T(8,128)} %land_in.1, s32[1,128]{1,0:T(1,128)} %bitcast.4), custom_call_target="tpu_custom_call" | custom-call | tf_op jit(solution)/shard_map/wave_window/pallas_call | solution.py:547
  31.3 2.2 %hand_over.1 = (f32[9216,128]{1,0:T(8,128)}, f32[4,8,128]{2,1,0:T(8,128)}) custom-call(f32[9216,128]{1,0:T(8,128)S(1)} %get-tuple-element.6.out, f32[16,2,128]{2,1,0:T(2,128)S(1)} %get-tuple-element.7.recv), custom_call_target="tpu_custom_call" | custom-call | tf_op jit(solution)/shard_map/hand_over/pallas_call | solution.py:595

commit v7 on v3

--- a/solution.py
+++ b/solution.py
@@ -530,7 +530,7 @@
         name="wave_window",
     )(*[pltpu.with_memory_space_constraint(a, pltpu.HBM) for a in (
         spectrum.reshape(cells, SUB, lats), wind, land_sea, band_rows.reshape(1, lats))])
-    parts = 4
+    parts = 1
     after, ocean = pl.pallas_call(
         functools.partial(finish_kernel, n, parts),
         out_shape=(jax.ShapeDtypeStruct((cells * SUB, lats), f32),

time: 33.7 us -> 33.7 us (level)
  no operation moved by 1% of the time
where the time goes in v7:
time: 33.7 us; the launch traced here: 33.6 us
  Pallas kernels  32.9 us (98%)
  between operations  0.64 us (2%)
    pallas_call x1, Pallas kernels, per_device(): pl.pallas_call(functools.partial(kernel, n, dirs, groups), out_shape=(plt...  30.7 us
    pallas_call x1, Pallas kernels, per_device(): pl.pallas_call(functools.partial(finish_kernel, n, parts), out_shape=(jax...  2.23 us

profile of v7, /device:TPU:0, one launch (start us, length us, event | category | flops | bytes accessed | tf_op | source)
XLA Modules:
  0.0 33.6 jit_solution(18215750813071460366)
XLA Ops:
  0.6 30.7 %wave_window.1 = (f32[9216,128]{1,0:T(8,128)S(1)}, f32[16,8,128]{2,1,0:T(8,128)S(1)}) custom-call(f32[1152,8,128]{2,1,0:T(8,128)} %bitcast.3, f32[2,8,128]{2,1,0:T(8,128)} %wind_in.1, s32[8,128]{1,0:T(8,128)} %land_in.1, s32[1,128]{1,0:T(1,128)} %bitcast.4), custom_call_target="tpu_custom_call" | custom-call | tf_op jit(solution)/shard_map/wave_window/pallas_call | solution.py:486
  31.3 2.2 %hand_over.1 = (f32[9216,128]{1,0:T(8,128)}, f32[4,8,128]{2,1,0:T(8,128)}) custom-call(f32[9216,128]{1,0:T(8,128)S(1)} %get-tuple-element.6.out, f32[16,8,128]{2,1,0:T(8,128)S(1)} %get-tuple-element.7.recv), custom_call_target="tpu_custom_call" | custom-call | tf_op jit(solution)/shard_map/hand_over/pallas_call | solution.py:534
